TPU v7x, 32 devices: a whole 2x2x4 slice. The times are simulated.
32 devices in a mesh: tp: 4 (over z), dp: 8 (over y, x, core).
Axes of the slice: x: 2, y: 2, z: 4, core: 2. Of those that a mesh axis runs over, the one named last changes fastest.
Arguments:
- w_in: float32 [2, 1024, 7168], P(None, None, 'tp')
- w_out: float32 [2, 5120, 1024], P(None, 'tp')
- g_in: float32 [8, 2, 1024, 7168], P('dp', None, None, 'tp')
- g_out: float32 [8, 2, 5120, 1024], P('dp', None, 'tp')
- m_in: bfloat16 [2, 1024, 7168], P(None, 'dp', 'tp')
- m_out: bfloat16 [2, 5120, 1024], P(None, 'tp', 'dp')
- r_in: float32 [2, 1024], P(None, 'dp')
- c_in: float32 [2, 7168], P(None, 'tp')
- r_out: float32 [2, 5120], P(None, 'tp')
- c_out: float32 [2, 1024], P(None, 'dp')
- learn_rate: float32 [], replicated
- weight_decay: float32 [], replicated
- beta_two: float32 [], replicated
Outputs:
- output 1: float32 [2, 1024, 7168], P(None, None, 'tp')
- output 2: float32 [2, 5120, 1024], P(None, 'tp')
- output 3: bfloat16 [2, 1024, 7168], P(None, 'dp', 'tp')
- output 4: bfloat16 [2, 5120, 1024], P(None, 'tp', 'dp')
- output 5: float32 [2, 1024], P(None, 'dp')
- output 6: float32 [2, 7168], P(None, 'tp')
- output 7: float32 [2, 5120], P(None, 'tp')
- output 8: float32 [2, 1024], P(None, 'dp')
All inputs are finite; a program needn't handle non-finite values.
Results may differ from a plain program's by a relative error of at most 0.00121581.
Values sent between devices are 32-bit elements.
A program may use at most 1 GiB of HBM per device.

v0:
```python
import jax
import jax.numpy as jnp
from jax import lax
from jax.sharding import PartitionSpec as P


def local_update(weight, grad_rep, moment, row_old, col_old, learn_rate, weight_decay, beta_two, row_axis, col_axis, row_devs, col_devs):
    dp_dim = 1 if row_axis == 'dp' else 2
    grad_part = lax.psum_scatter(grad_rep[0], 'dp', scatter_dimension=dp_dim, tiled=True)
    n_rows = grad_part.shape[1] * row_devs
    n_cols = grad_part.shape[2] * col_devs
    grad_sq = grad_part * grad_part + 1e-30
    row_mean = lax.psum(jnp.sum(grad_sq, axis=2), col_axis) / n_cols
    col_mean = lax.psum(jnp.sum(grad_sq, axis=1), row_axis) / n_rows
    row_new = beta_two * row_old + (1.0 - beta_two) * row_mean
    col_new = beta_two * col_old + (1.0 - beta_two) * col_mean
    row_avg = lax.psum(jnp.sum(row_new, axis=1), row_axis) / n_rows
    second = row_new[:, :, None] * col_new[:, None, :] / row_avg[:, None, None]
    update = grad_part / jnp.sqrt(second)
    total_sq = lax.psum(jnp.sum(update * update, axis=(1, 2)), ('tp', 'dp'))
    rms_val = jnp.sqrt(total_sq / (n_rows * n_cols))
    update = update / jnp.maximum(1.0, rms_val)[:, None, None]
    mom_new = (0.9 * moment.astype(jnp.float32) + 0.1 * update).astype(jnp.bfloat16)
    width = grad_part.shape[dp_dim]
    w_block = lax.dynamic_slice_in_dim(weight, lax.axis_index('dp') * width, width, axis=dp_dim)
    w_block = w_block - learn_rate * mom_new.astype(jnp.float32) - learn_rate * weight_decay * w_block
    w_new = lax.all_gather(w_block, 'dp', axis=dp_dim, tiled=True)
    return w_new, mom_new, row_new, col_new


def solution(mesh):
    tp_devs = mesh.shape['tp']
    dp_devs = mesh.shape['dp']

    def body(w_in, w_out, g_in, g_out, m_in, m_out, r_in, c_in, r_out, c_out, learn_rate, weight_decay, beta_two):
        in_result = local_update(w_in, g_in, m_in, r_in, c_in, learn_rate, weight_decay, beta_two, 'dp', 'tp', dp_devs, tp_devs)
        out_result = local_update(w_out, g_out, m_out, r_out, c_out, learn_rate, weight_decay, beta_two, 'tp', 'dp', tp_devs, dp_devs)
        return (in_result[0], out_result[0], in_result[1], out_result[1], in_result[2], in_result[3], out_result[2], out_result[3])

    in_specs = (P(None, None, 'tp'), P(None, 'tp', None), P('dp', None, None, 'tp'), P('dp', None, 'tp', None), P(None, 'dp', 'tp'), P(None, 'tp', 'dp'), P(None, 'dp'), P(None, 'tp'), P(None, 'tp'), P(None, 'dp'), P(), P(), P())
    out_specs = (P(None, None, 'tp'), P(None, 'tp', None), P(None, 'dp', 'tp'), P(None, 'tp', 'dp'), P(None, 'dp'), P(None, 'tp'), P(None, 'tp'), P(None, 'dp'))
    return jax.shard_map(body, mesh=mesh, in_specs=in_specs, out_specs=out_specs, check_vma=False)
```

profile of v0, /device:TPU:0, one launch (start us, length us, event | category | flops | bytes accessed | tf_op | source)
XLA Modules:
  0.0 465.0 jit_solution(8234183247008817625)
XLA Ops:
  7.2 0.0 reduce-scatter.5.cloned.1.call-start
  7.2 0.7 reduce-scatter.5.cloned.1.call-update
  7.9 0.0 reduce-scatter.3.cloned.1.call-start
  7.9 0.7 reduce-scatter.3.cloned.1.call-update
  8.7 0.0 copy-start.9
  8.7 0.0 copy-start.6
  8.7 0.0 copy-start.5
  8.7 0.0 copy-start.10
  8.7 0.0 all-gather.5.cloned.1.call-start
  10.7 84.4 %reduce-scatter.5.cloned.1.call-done = f32[2,1280,128]{2,1,0:T(8,128)} async-done(((f32[2,1280,1024]{2,1,0:T(8,128)}), f32[2,1280,128]{2,1,0:T(8,128)}) %reduce-scatter.5.cloned.1.call-update) | async-done | bytes 1310736 | tf_op jit(solution)/shard_map/reduce_scatter | solution.py:9
  95.1 0.0 copy-start.1
  95.1 1.8 fusion.2
  96.9 102.5 %reduce-scatter.3.cloned.1.call-done = f32[2,128,1792]{2,1,0:T(8,128)} async-done(((f32[2,1024,1792]{2,1,0:T(8,128)}), f32[2,128,1792]{2,1,0:T(8,128)}) %reduce-scatter.3.cloned.1.call-update) | async-done | bytes 1835024 | tf_op jit(solution)/shard_map/reduce_scatter | solution.py:9
  199.4 0.0 copy-start
  199.4 2.0 fusion
  201.4 11.7 %psum.56 = f32[2,128]{1,0:T(2,128)S(1)} all-reduce(f32[2,128]{1,0:T(2,128)S(1)} %get-tuple-element.9), channel_id=1, replica_groups=mesh['tp'=4,'dp'=8] {'tp'}, use_global_device_ids=true, to_apply=%region_2.0 | all-reduce | flops 256 | bytes 2048 | tf_op jit(solution)/shard_map/psum | solution.py:13
  213.1 0.0 copy-done.9
  213.1 0.1 fusion.5
  213.2 0.0 copy-start.7
  213.2 22.4 %all-reduce.1 = (f32[2]{0:T(128)S(1)}, f32[2,1792]{1,0:T(2,128)S(1)}, f32[2,1280]{1,0:T(2,128)S(1)}) all-reduce(f32[2]{0:T(128)S(1)} %get-tuple-element.25, f32[2,1792]{1,0:T(2,128)S(1)} %get-tuple-element.8, f32[2,1280]{1,0:T(2,128)S(1)} %get-tuple-element.11), channel_id=1, replica_groups=mesh['tp'=4,'dp'=8] {'dp'}, use_global_device_ids=true, to_apply=%region_6.0 | all-reduce | flops 6146 | bytes 49168 | tf_op jit(solution)/shard_map/psum | solution.py:17
  235.6 0.0 copy-done.6
  235.6 0.1 fusion.4
  235.8 0.0 copy-start.4
  235.8 8.4 %all-reduce.2 = (f32[2]{0:T(128)S(1)}, f32[2,128]{1,0:T(2,128)S(1)}) all-reduce(f32[2]{0:T(128)S(1)} %get-tuple-element.23, f32[2,128]{1,0:T(2,128)S(1)} %get-tuple-element.10), channel_id=1, replica_groups=mesh['tp'=4,'dp'=8] {'tp'}, use_global_device_ids=true, to_apply=%region_15.0 | all-reduce | flops 258 | bytes 2064 | tf_op jit(solution)/shard_map/psum | solution.py:17
  244.2 0.0 copy-done.5
  244.2 0.0 copy-start.3
  244.2 0.0 copy-done.10
  244.2 0.0 copy-start.8
  244.2 0.0 copy-done.1
  244.2 0.5 multiply_reduce_fusion.1
  244.7 0.0 copy-done
  244.7 0.7 multiply_reduce_fusion
  245.4 39.6 %all-reduce = (f32[2]{0:T(128)S(1)}, f32[2]{0:T(128)S(1)}) all-reduce(f32[2]{0:T(128)S(1)} %multiply_reduce_fusion, f32[2]{0:T(128)S(1)} %multiply_reduce_fusion.1), channel_id=1, replica_groups=mesh['tp'=4,'dp'=8] {'tp','dp'}, use_global_device_ids=true, to_apply=%region_8.0 | all-reduce | flops 4 | bytes 32 | tf_op jit(solution)/shard_map/psum | solution.py:20
  285.0 3.4 multiply_subtract_fusion.1
  288.5 0.0 copy-done.4
  288.5 0.0 copy-done.8
  288.5 0.0 copy-start.2
  288.5 0.0 all-gather.5.cloned.1.call-update
  288.5 0.0 all-gather.3.cloned.1.call-start
  288.6 0.0 copy-done.7
  288.6 0.0 copy-done.3
  288.6 1.1 copy-done.2
  289.7 3.9 multiply_subtract_fusion
  293.6 0.0 all-gather.3.cloned.1.call-update
  293.6 60.0 %all-gather.5.cloned.1.call-done = f32[2,1280,1024]{2,1,0:T(8,128)} async-done(((f32[2,1280,128]{2,1,0:T(8,128)}), f32[2,1280,1024]{2,1,0:T(8,128)}) %all-gather.5.cloned.1.call-update) | async-done | bytes 10485776 | tf_op jit(solution)/shard_map/all_gather | solution.py:27
  353.6 83.1 %all-gather.3.cloned.1.call-done = f32[2,1024,1792]{2,1,0:T(8,128)} async-done(((f32[2,128,1792]{2,1,0:T(8,128)}), f32[2,1024,1792]{2,1,0:T(8,128)}) %all-gather.3.cloned.1.call-update) | async-done | bytes 14680080 | tf_op jit(solution)/shard_map/all_gather | solution.py:27
  436.7 11.6 %copy.26 = f32[2,1024,1792]{2,1,0:T(8,128)} copy(f32[2,1024,1792]{2,1,0:T(8,128)} %all-gather.3.cloned.1.call-done) | data formatting | bytes 29360128
  448.2 10.3 %copy.27 = f32[2,1280,1024]{2,1,0:T(8,128)} copy(f32[2,1280,1024]{2,1,0:T(8,128)} %all-gather.5.cloned.1.call-done) | data formatting | bytes 20971520
  (5 shorter events, 0.0 us)
Async XLA Ops:
  7.2 87.9 %reduce-scatter.5.cloned.1.call-start = ((), (), s32[]{:S(2)}) async-start(), calls=%async_computation.4 | async-start | bytes 11796480 | tf_op jit(solution)/shard_map/reduce_scatter | solution.py:9
  7.9 191.5 %reduce-scatter.3.cloned.1.call-start = ((), (), s32[]{:S(2)}) async-start(), calls=%async_computation.2 | async-start | bytes 16515072 | tf_op jit(solution)/shard_map/reduce_scatter | solution.py:9
  8.7 204.4 %copy-start.9 = (f32[2,128]{1,0:T(2,128)S(1)}, f32[2,128]{1,0:T(2,128)}, u32[]{:S(2)}) copy-start(f32[2,128]{1,0:T(2,128)} %param.19) | copy-start | bytes 3076
  8.7 227.0 %copy-start.6 = (f32[2,1280]{1,0:T(2,128)S(1)}, f32[2,1280]{1,0:T(2,128)}, u32[]{:S(2)}) copy-start(f32[2,1280]{1,0:T(2,128)} %param.21) | copy-start | bytes 30724
  8.7 235.5 %copy-start.5 = (f32[2,1792]{1,0:T(2,128)S(1)}, f32[2,1792]{1,0:T(2,128)}, u32[]{:S(2)}) copy-start(f32[2,1792]{1,0:T(2,128)} %param.20) | copy-start | bytes 43012
  8.7 235.5 %copy-start.10 = (f32[2,128]{1,0:T(2,128)S(1)}, f32[2,128]{1,0:T(2,128)}, u32[]{:S(2)}) copy-start(f32[2,128]{1,0:T(2,128)} %param.22) | copy-start | bytes 3076
  8.7 344.9 %all-gather.5.cloned.1.call-start = ((), (), s32[]{:S(2)}) async-start(), calls=%async_computation.5 | async-start | bytes 11796480 | tf_op jit(solution)/shard_map/all_gather | solution.py:27
  95.1 149.2 %copy-start.1 = (f32[2,1280,128]{2,1,0:T(8,128)S(1)}, f32[2,1280,128]{2,1,0:T(8,128)}, u32[]{:S(2)}) copy-start(f32[2,1280,128]{2,1,0:T(8,128)} %reduce-scatter.5.cloned.1.call-done) | copy-start | bytes 3932164
  199.4 45.3 %copy-start = (f32[2,128,1792]{2,1,0:T(8,128)S(1)}, f32[2,128,1792]{2,1,0:T(8,128)}, u32[]{:S(2)}) copy-start(f32[2,128,1792]{2,1,0:T(8,128)} %reduce-scatter.3.cloned.1.call-done) | copy-start | bytes 5505028
  213.2 75.3 %copy-start.7 = (f32[2,128]{1,0:T(2,128)}, f32[2,128]{1,0:T(2,128)S(1)}, u32[]{:S(2)}) copy-start(f32[2,128]{1,0:T(2,128)S(1)} %get-tuple-element.41) | copy-start | bytes 3076
  235.8 52.7 %copy-start.4 = (f32[2,1280]{1,0:T(2,128)}, f32[2,1280]{1,0:T(2,128)S(1)}, u32[]{:S(2)}) copy-start(f32[2,1280]{1,0:T(2,128)S(1)} %get-tuple-element.43) | copy-start | bytes 30724
  244.2 44.4 %copy-start.3 = (f32[2,1792]{1,0:T(2,128)}, f32[2,1792]{1,0:T(2,128)S(1)}, u32[]{:S(2)}) copy-start(f32[2,1792]{1,0:T(2,128)S(1)} %multiply_add_fusion.2) | copy-start | bytes 43012
  244.2 44.3 %copy-start.8 = (f32[2,128]{1,0:T(2,128)}, f32[2,128]{1,0:T(2,128)S(1)}, u32[]{:S(2)}) copy-start(f32[2,128]{1,0:T(2,128)S(1)} %multiply_add_fusion.4) | copy-start | bytes 3076
  288.5 1.2 copy-start.2
  288.5 148.2 %all-gather.3.cloned.1.call-start = ((), (), s32[]{:S(2)}) async-start(), calls=%async_computation.3 | async-start | bytes 16515072 | tf_op jit(solution)/shard_map/all_gather | solution.py:27
Sparse Core Ops, SparseCore 0:
  11.5 83.5 reduce-scatter.4
  98.6 100.8 reduce-scatter.2
  288.6 64.8 all-gather.4
  355.9 80.7 all-gather.2
where the time goes:
time: 466 us; the launch traced here: 465 us
  waiting for transfers between devices  331 us (71%)
  blocking collectives  82.1 us (18%)
  local copies, waits for them, and re-layouts  23 us (5%)
  between operations  15.8 us (3%)
  other arithmetic  12.6 us (3%)
    reduce_scatter x2, waiting for transfers between devices, local_update(): lax.psum_scatter(grad_rep[0], 'dp', scatter_dimension=dp_dim, tiled=True)  187 us
    all_gather x2, waiting for transfers between devices, local_update(): w_new = lax.all_gather(w_block, 'dp', axis=dp_dim, tiled=True)  143 us
    psum x1, blocking collectives, local_update(): total_sq = lax.psum(jnp.sum(update * update, axis=(1, 2)), ('tp', 'dp'))  39.6 us
    psum x2, blocking collectives, local_update(): row_avg = lax.psum(jnp.sum(row_new, axis=1), row_axis) / n_rows  30.8 us
    unnamed x24, local copies, waits for them, and re-layouts  23 us
    psum x1, blocking collectives, local_update(): row_mean = lax.psum(jnp.sum(grad_sq, axis=2), col_axis) / n_cols  11.7 us
  transfers between devices with their start and end apart: 4, of which 4 were waited for; matrix products, arithmetic and copies ran while one was open for 1% of the time, Pallas kernels for 0%

commit v1 on v0

v1 whole, which is shorter than its diff:
```python
import jax
import jax.numpy as jnp
from jax import lax
from jax.experimental import pallas as pl
from jax.experimental.pallas import tpu as pltpu
from jax.sharding import PartitionSpec as P

MESH = pl.DeviceIdType.MESH
F32 = jnp.float32
LANES = 128
TP, DP = 4, 8
PARTS = 4
STORES = 4


def total(x):
    return jnp.sum(jnp.sum(x, axis=0, keepdims=True), axis=1, keepdims=True)


def eye_mask():
    row = lax.broadcasted_iota(jnp.int32, (LANES, LANES), 0)
    col = lax.broadcasted_iota(jnp.int32, (LANES, LANES), 1)
    return row == col


def to_row(col):
    return jnp.sum(jnp.where(eye_mask(), jnp.broadcast_to(col, (LANES, LANES)), 0.0), axis=0, keepdims=True)


def to_rows(row):
    col = jnp.sum(jnp.where(eye_mask(), jnp.broadcast_to(row, (LANES, LANES)), 0.0), axis=1, keepdims=True)
    return jnp.broadcast_to(col, (LANES, LANES))


def fused_kernel(g_in, g_out, w_in, w_out, m_in, m_out, r_in, c_in, r_out, c_out, lr_ref, wd_ref, b2_ref,
                 ow_in, ow_out, om_in, om_out, or_in, oc_in, or_out, oc_out,
                 gm_in, gm_out, r1_in, r1_out, r2_in, r2_out, ws_in, ws_out,
                 vr_in, vc_in, vr_out, vc_out, vp_in, vp_out, vh_in, vh_out, vf_in, vf_out, ts, tr, rp, rc, short, olds, rb,
                 ld_sem, pre_sem, st_sem, sm_sem, d2_send, d2_first, d2_recv, p1_send, p1_recv, p2_send, p2_recv,
                 a_send, a1_recv, a2_recv, a2_last, ad_send, ad_recv, v_send, v_recv, z_sem):
    t = lax.axis_index('tp')
    d = lax.axis_index('dp')
    core = lax.rem(d, 2)
    chip = d // 2
    x = lax.rem(chip, 2)
    y = chip // 2
    k_own = chip
    k_x = y * 2 + (1 - x)
    k_y = (1 - y) * 2 + x
    k_d = (1 - y) * 2 + (1 - x)
    dev_x = k_x * 2 + core
    dev_y = k_y * 2 + core
    dev_d = k_d * 2 + core
    dev_c = chip * 2 + (1 - core)
    lr = lr_ref[0]
    wd = wd_ref[0]
    b2 = b2_ref[0]
    n_layers = gm_in.shape[0]
    mats = [(0, i) for i in range(n_layers)] + [(1, i) for i in range(n_layers)]
    n_mats = len(mats)
    sw = gm_in.shape[2]
    half_in = sw // 2
    cols_in = gm_in.shape[3]
    rows_out = gm_out.shape[2]
    half_out = rows_out // 2

    def full_view(refs, mat, q, h, lead):
        kind, l = mat
        pre = (0,) if lead else ()
        if kind == 0:
            return refs[0].at[pre + (l, pl.ds(pl.multiple_of(q * sw + h * half_in, half_in), half_in), slice(None))]
        return refs[1].at[pre + (l, pl.ds(h * half_out, half_out), pl.ds(pl.multiple_of(q * LANES, LANES), LANES))]

    def full_shard(refs, mat, q):
        kind, l = mat
        if kind == 0:
            return refs[0].at[l, pl.ds(pl.multiple_of(q * sw, sw), sw), :]
        return refs[1].at[l, :, pl.ds(pl.multiple_of(q * LANES, LANES), LANES)]

    def half_view(refs, mat, k, h):
        kind, l = mat
        size = half_in if kind == 0 else half_out
        return refs[kind].at[l, k, pl.ds(h * size, size)]

    gs = (g_in, g_out)
    ows = (ow_in, ow_out)
    gms = (gm_in, gm_out)
    r1s = (r1_in, r1_out)
    r2s = (r2_in, r2_out)
    oms = (om_in, om_out)
    wss = (ws_in, ws_out)

    def remote(src, dst, send, recv, dev_t, dev_d):
        cp = pltpu.make_async_remote_copy(src_ref=src, dst_ref=dst, send_sem=send, recv_sem=recv,
                                          device_id=(dev_t, dev_d), device_id_type=MESH)
        cp.start()
        return cp

    def wait_bytes(ref, sem):
        pltpu.make_async_copy(ref, ref, sem).wait()

    def add_into(dst, src):
        rows, cols = dst.shape
        step = 8 if cols > LANES else 128
        if rows % step:
            step = 8

        def body(i, carry):
            sl = pl.ds(pl.multiple_of(i * step, step), step)
            dst[sl, :] = dst[sl, :] + src[sl, :]
            return carry

        lax.fori_loop(0, rows // step, body, 0)

    pieces = [(k_d, 0), (k_d, 1), (k_x, 0), (k_y, 1), (k_y, 0), (k_x, 1), (k_own, 0), (k_own, 1)]
    routes = [(0, 1, dev_x), (1, 1, dev_y), (0, 0, dev_x), (1, 0, dev_y)]

    def sub(ref, i):
        rows = ref.shape[0] // PARTS
        return ref.at[pl.ds(i * rows, rows)]

    def start_loads(m):
        mat = mats[m]
        for i, (k, h) in enumerate(pieces):
            sem = ld_sem.at[min(i, 2)] if m == 0 else ld_sem.at[2 + m]
            pltpu.make_async_copy(full_view(gs, mat, 2 * k + core, h, True), half_view(gms, mat, k, h), sem).start()

    def start_preload():
        for i, (k, h) in enumerate(pieces):
            q = 2 * k + (1 - core)
            pltpu.make_async_copy(full_view(gs, mats[0], q, h, True), full_view(ows, mats[0], q, h, False), pre_sem.at[min(i, 2)]).start()

    def swap_first():
        views = [full_view(ows, mats[0], 2 * k + (1 - core), h, False) for k, h in pieces]
        for i in range(2):
            wait_bytes(views[i], pre_sem.at[i])
            remote(sub(views[i], 0), sub(views[i], 0), d2_send.at[2], d2_first.at[i, 0], t, dev_c)
        for p in range(1, PARTS):
            for i in range(2):
                remote(sub(views[i], p), sub(views[i], p), d2_send.at[2], d2_first.at[i, p], t, dev_c)
        wait_bytes(gm_in.at[0, pl.ds(0, 3)], pre_sem.at[2])
        for i in range(2, 8):
            remote(views[i], views[i], d2_send.at[2], d2_recv.at[min(i - 2, 2)], t, dev_c)

    def start_swap(m):
        mat = mats[m]
        for k, h in pieces:
            q = 2 * k + (1 - core)
            remote(full_view(gs, mat, q, h, True), full_view(ows, mat, q, h, False), d2_send.at[mat[0]], d2_recv.at[2 + m], t, dev_c)

    def chip_views(m, i):
        k, h = pieces[i]
        return half_view(gms, mats[m], k, h), full_view(ows, mats[m], 2 * k + core, h, False)

    def send_first(m, i, part=None):
        kind, l = mats[m]
        h, j, dev = routes[i]
        mine, other = chip_views(m, i)
        dst = r1s[kind].at[l, h, j]
        if part is not None:
            mine, other, dst = sub(mine, part), sub(other, part), sub(dst, part)
        add_into(mine, other)
        remote(mine, dst, p1_send.at[kind], p1_recv.at[m, 2 * h + j], t, dev)

    def stage_a_first():
        views = [chip_views(0, i)[0] for i in range(8)]
        for i in range(2):
            wait_bytes(views[i], ld_sem.at[i])
        for p in range(PARTS):
            for i in range(2):
                wait_bytes(sub(views[i], p), d2_first.at[i, p])
                send_first(0, i, p)
        wait_bytes(gm_in.at[0, pl.ds(0, 3)], ld_sem.at[2])
        for i in range(2, 4):
            wait_bytes(views[i], d2_recv.at[i - 2])
            send_first(0, i)

    def keep_first(m):
        for i in range(4, 8):
            add_into(*chip_views(m, i))

    def stage_a(m):
        kind, l = mats[m]
        gm = gms[kind].at[l]
        wait_bytes(gm, ld_sem.at[2 + m])
        wait_bytes(gm, d2_recv.at[2 + m])
        for i in range(4):
            send_first(m, i)
        keep_first(m)

    def stage_b(m):
        kind, l = mats[m]
        for h, k, dev in ((0, k_y, dev_y), (1, k_x, dev_x)):
            mine = half_view(gms, mats[m], k, h)
            wait_bytes(mine, p1_recv.at[m, 2 * h + 1])
            add_into(mine, r1s[kind].at[l, h, 1])
            remote(mine, r2s[kind].at[l, h], p2_send.at[kind], p2_recv.at[m, h], t, dev)
        for h in range(2):
            mine = half_view(gms, mats[m], k_own, h)
            wait_bytes(mine, p1_recv.at[m, 2 * h])
            add_into(mine, r1s[kind].at[l, h, 0])

    vps = (vp_in, vp_out)
    vhs = (vh_in, vh_out)
    vfs = (vf_in, vf_out)

    def send_chips(slots, send, recv):
        for dev in (dev_x, dev_y, dev_d):
            remote(slots.at[chip], slots.at[chip], send, recv, t, dev)

    def send_core(slots, send, recv):
        remote(slots.at[core], slots.at[core], send, recv, t, dev_c)

    def send_tp(slots, send, recv):
        for i in range(1, TP):
            remote(slots.at[t], slots.at[t], send, recv, lax.rem(t + i, TP), d)

    def sum_slots(slots, count):
        acc = slots[0]
        for i in range(1, count):
            acc = acc + slots[i]
        return acc

    def stage_c(m):
        kind, l = mats[m]
        mat = mats[m]
        for h in range(2):
            mine = half_view(gms, mat, k_own, h)
            wait_bytes(mine, p2_recv.at[m, h])
            add_into(mine, r2s[kind].at[l, h])
        own = vps[kind].at[l, core]
        shard = gms[kind].at[l, k_own]
        if kind == 0:
            def body(i, acc):
                sl = pl.ds(pl.multiple_of(i * 8, 8), 8)
                g = shard[sl, :]
                s = g * g + 1e-30
                rb[sl, :] = jnp.broadcast_to(jnp.sum(s, axis=1, keepdims=True), (8, LANES))
                return acc + s

            acc = lax.fori_loop(0, sw // 8, body, jnp.zeros((8, cols_in), F32))
            own[:, pl.ds(0, cols_in)] = jnp.sum(acc, axis=0, keepdims=True)
            own[:, pl.ds(cols_in, LANES)] = vr_in[pl.ds(l, 1), :]
            spare = own.shape[1] - cols_in - LANES
            if spare:
                own[:, pl.ds(cols_in + LANES, spare)] = jnp.zeros((1, spare), F32)
            short[pl.ds(m, 1), :] = to_row(rb[pl.ds(0, LANES), 0:1])
        else:
            def body(i, acc):
                g = shard[pl.ds(pl.multiple_of(i * LANES, LANES), LANES), :]
                s = g * g + 1e-30
                own[:, pl.ds(pl.multiple_of(i * LANES, LANES), LANES)] = to_row(jnp.sum(s, axis=1, keepdims=True))
                return acc + jnp.sum(s, axis=0, keepdims=True)

            short[pl.ds(m, 1), :] = lax.fori_loop(0, rows_out // LANES, body, jnp.zeros((1, LANES), F32))
        send_core(vps[kind].at[l], v_send.at[kind], v_recv.at[m, 0])

    def stage_k(m):
        kind, l = mats[m]
        both = vps[kind].at[l]
        wait_bytes(both.at[0], v_recv.at[m, 0])
        size = vhs[kind].shape[3]
        half = pl.ds(pl.multiple_of(core * size, LANES), size)
        vhs[kind].at[l, chip][...] = both.at[0][:, half] + both.at[1][:, half]
        send_chips(vhs[kind].at[l], v_send.at[2 + kind], v_recv.at[m, 1])

    def stage_d(m):
        kind, l = mats[m]
        slots = vhs[kind].at[l]
        wait_bytes(slots.at[pl.ds(0, 3)], v_recv.at[m, 1])
        vfs[kind].at[l, core][...] = sum_slots(slots, 4)
        send_core(vfs[kind].at[l], v_send.at[4 + kind], v_recv.at[m, 2])

    in_rows, in_cols = sw * DP, cols_in * TP
    out_rows, out_cols = rows_out * TP, sw * DP

    def stage_l(m):
        kind, l = mats[m]
        both = vfs[kind].at[l]
        wait_bytes(both.at[0], v_recv.at[m, 2])
        acc = jnp.concatenate([both[0], both[1]], axis=1)
        own = ts.at[m, t]
        own[:, pl.ds(0, LANES)] = short[pl.ds(m, 1), :]
        if kind == 0:
            col_sum = acc[:, :cols_in]
            oc_in[pl.ds(l, 1), :] = b2 * vc_in[pl.ds(l, 1), :] + (1.0 - b2) * (col_sum / in_rows)
            plane = jnp.sum(col_sum, axis=1, keepdims=True)
            olds[pl.ds(l, 1), :] = acc[:, cols_in:cols_in + LANES]
        else:
            r_new = b2 * vr_out[pl.ds(l, 1), :] + (1.0 - b2) * (acc / out_cols)
            or_out[pl.ds(l, 1), :] = r_new
            plane = jnp.sum(r_new, axis=1, keepdims=True)
        own[:, pl.ds(LANES, LANES)] = jnp.broadcast_to(plane, (1, LANES))
        send_tp(ts.at[m], v_send.at[6], v_recv.at[m, 3])

    def stage_e(m):
        kind, l = mats[m]
        wait_bytes(ts.at[m, pl.ds(0, TP - 1)], v_recv.at[m, 3])
        acc = sum_slots(ts.at[m], TP)
        vec = acc[:, :LANES]
        tot = acc[:, LANES:LANES + 1]
        shard = gms[kind].at[l, k_own]
        if kind == 0:
            r_new = b2 * vr_in[pl.ds(l, 1), :] + (1.0 - b2) * (vec / in_cols)
            or_in[pl.ds(l, 1), :] = r_new
            old = jnp.sum(olds[pl.ds(l, 1), :], axis=1, keepdims=True)
            avg = (b2 * old + (1.0 - b2) * (tot / in_cols)) / in_rows
            rb[pl.ds(0, LANES), :] = to_rows(1.0 / jnp.sqrt(r_new))
            cj = jnp.sqrt(avg) / jnp.sqrt(oc_in[pl.ds(l, 1), :])

            def body(i, acc):
                sl = pl.ds(pl.multiple_of(i * 8, 8), 8)
                u = (shard[sl, :] * rb[sl, 0:1]) * cj
                shard[sl, :] = u
                return acc + u * u

            sq = lax.fori_loop(0, sw // 8, body, jnp.zeros((8, cols_in), F32))
        else:
            c_new = b2 * vc_out[pl.ds(l, 1), :] + (1.0 - b2) * (vec / out_rows)
            oc_out[pl.ds(l, 1), :] = c_new
            avg = tot / out_rows
            cj = jnp.sqrt(avg) / jnp.sqrt(c_new)

            def body(i, acc):
                sl = pl.ds(pl.multiple_of(i * LANES, LANES), LANES)
                ri = to_rows(1.0 / jnp.sqrt(or_out[pl.ds(l, 1), sl]))
                u = (shard[sl, :] * ri) * cj
                shard[sl, :] = u
                return acc + u * u

            sq = lax.fori_loop(0, rows_out // LANES, body, jnp.zeros((LANES, LANES), F32))
        tr.at[m, t][...] = jnp.broadcast_to(total(sq), (1, LANES))
        send_tp(tr.at[m], v_send.at[7], v_recv.at[m, 4])

    def stage_f(m):
        wait_bytes(tr.at[m, pl.ds(0, TP - 1)], v_recv.at[m, 4])
        rp.at[m, core][...] = sum_slots(tr.at[m], TP)
        send_core(rp.at[m], v_send.at[8], v_recv.at[m, 5])

    def stage_n(m):
        wait_bytes(rp.at[m, 0], v_recv.at[m, 5])
        rc.at[m, chip][...] = rp.at[m][0] + rp.at[m][1]
        send_chips(rc.at[m], v_send.at[9], v_recv.at[m, 6])

    def stage_g(m):
        mat = mats[m]
        kind, l = mat
        wait_bytes(rc.at[m, pl.ds(0, 3)], v_recv.at[m, 6])
        size = float(in_rows * in_cols if kind == 0 else out_rows * out_cols)
        rms = jnp.sqrt(sum_slots(rc.at[m], 4) / size)
        scale = (1.0 / jnp.maximum(1.0, rms))[:, 0:1]
        shard = gms[kind].at[l, k_own]
        mom = oms[kind].at[l]
        old = wss[kind].at[l]
        new = full_shard(ows, mat, d)
        if l == 0:
            wait_bytes(oms[kind], st_sem.at[kind, 0])
            wait_bytes(wss[kind], st_sem.at[kind, 1])
        step = 16 if kind == 0 else 128

        def body(i, carry):
            sl = pl.ds(pl.multiple_of(i * step, step), step)
            mn = (0.9 * mom[sl, :].astype(F32) + 0.1 * (shard[sl, :] * scale)).astype(jnp.bfloat16)
            mom[sl, :] = mn
            w = old[sl, :]
            new[sl, :] = w - lr * mn.astype(F32) - lr * wd * w
            return carry

        lax.fori_loop(0, shard.shape[0] // step, body, 0)
        q = d
        a = full_view(ows, mat, q, 0, False)
        b = full_view(ows, mat, q, 1, False)
        remote(a, a, a_send.at[kind], a1_recv.at[m, 0], t, dev_y)
        remote(b, b, a_send.at[kind], a1_recv.at[m, 1], t, dev_x)
        remote(a, a, a_send.at[kind], a2_recv.at[m, 0], t, dev_x)
        remote(b, b, a_send.at[kind], a2_recv.at[m, 1], t, dev_y)
        pass_core(m, new)

    def pass_core(m, view):
        kind = mats[m][0]
        remote(view, view, ad_send.at[kind], ad_recv.at[kind], t, dev_c)

    def stage_h(m):
        mat = mats[m]
        kind = mat[0]
        a = full_view(ows, mat, 2 * k_y + core, 0, False)
        b = full_view(ows, mat, 2 * k_x + core, 1, False)
        for i, (view, dev) in enumerate(((a, dev_x), (b, dev_y))):
            wait_bytes(view, a1_recv.at[m, i])
            if m < n_mats - 1:
                remote(view, view, a_send.at[kind], a2_recv.at[m, 2 + i], t, dev)
            else:
                for p in range(PARTS):
                    remote(sub(view, p), sub(view, p), a_send.at[kind], a2_last.at[i, p], t, dev)
        pass_core(m, a)
        pass_core(m, b)

    def stage_i(m):
        last = m == n_mats - 1
        for i, k, h in ((0, k_x, 0), (1, k_y, 1)):
            view = full_view(ows, mats[m], 2 * k + core, h, False)
            wait_bytes(view, a2_recv.at[m, i])
            pass_core(m, view)
        views = [full_view(ows, mats[m], 2 * k_d + core, h, False) for h in range(2)]
        if not last:
            for i in range(2):
                wait_bytes(views[i], a2_recv.at[m, 2 + i])
                pass_core(m, views[i])
        else:
            for p in range(PARTS):
                for i in range(2):
                    wait_bytes(sub(views[i], p), a2_last.at[i, p])
                    pass_core(m, sub(views[i], p))

    small = [(r_in, vr_in), (c_in, vc_in), (r_out, vr_out), (c_out, vc_out)]
    barrier = pltpu.get_barrier_semaphore()
    z_near = jnp.minimum(t, 1) + jnp.minimum(TP - 1 - t, 1)

    def signal_z(sem):
        @pl.when(t > 0)
        def _():
            pl.semaphore_signal(sem, inc=1, device_id=(t - 1, d), device_id_type=MESH)

        @pl.when(t < TP - 1)
        def _():
            pl.semaphore_signal(sem, inc=1, device_id=(t + 1, d), device_id_type=MESH)

    for dev in (dev_x, dev_y, dev_c):
        pl.semaphore_signal(barrier, inc=1, device_id=(t, dev), device_id_type=MESH)
    signal_z(barrier)
    start_preload()
    start_loads(0)
    pl.semaphore_wait(barrier, 3 + z_near)
    swap_first()
    stage_a_first()
    start_loads(1)
    start_swap(1)
    signal_z(z_sem.at[0])
    wait_bytes(gm_in.at[0, pl.ds(0, 2)], d2_recv.at[2])
    keep_first(0)
    stage_a(1)
    for i, (src, dst) in enumerate(small):
        pltpu.make_async_copy(src, dst, sm_sem.at[i]).start()
    for m, (kind, l) in enumerate(mats):
        pltpu.make_async_copy((m_in, m_out)[kind].at[l], oms[kind].at[l], st_sem.at[kind, 0]).start()
        src = w_in.at[l, pl.ds(pl.multiple_of(d * sw, sw), sw), :] if kind == 0 else w_out.at[l, :, pl.ds(pl.multiple_of(d * LANES, LANES), LANES)]
        pltpu.make_async_copy(src, wss[kind].at[l], st_sem.at[kind, 1]).start()
    wait_bytes(gm_in.at[0], d2_send.at[2])
    pl.semaphore_wait(z_sem.at[0], z_near)
    signal_z(z_sem.at[1])
    for i, (src, dst) in enumerate(small):
        wait_bytes(dst, sm_sem.at[i])
    order = 's2 b0 a2 s3 b1 c0 k0 a3 b2 c1 k1 d0 l0 e0 f0 n0 b3 c2 k2 g0 d1 l1 e1 f1 n1 c3 k3 d2 l2 h0 e2 f2 n2 g1 i0 d3 l3 e3 f3 n3 h1 g2 i1 h2 g3 i2 h3 i3'
    def stage_s(m):
        start_loads(m)
        start_swap(m)

    stages = dict(s=stage_s, a=stage_a, b=stage_b, c=stage_c, d=stage_d, e=stage_e, f=stage_f, g=stage_g, h=stage_h, i=stage_i, k=stage_k, l=stage_l, n=stage_n)
    pl.semaphore_wait(z_sem.at[1], z_near)
    for item in order.split():
        stages[item[0]](int(item[1]))
    for kind in range(2):
        gm = gms[kind]
        wait_bytes(gm, ad_recv.at[kind])
        wait_bytes(gm.at[pl.ds(0, n_layers - 1 + kind)], d2_send.at[kind])
        wait_bytes(r1s[kind], p1_send.at[kind])
        wait_bytes(r2s[kind], p2_send.at[kind])
        wait_bytes(gm.at[:, pl.ds(0, 3)], a_send.at[kind])
        wait_bytes(gm, ad_send.at[kind])
        wait_bytes(vps[kind].at[pl.ds(0, n_layers), 0], v_send.at[kind])
        wait_bytes(vhs[kind].at[pl.ds(0, n_layers), pl.ds(0, 3)], v_send.at[2 + kind])
        wait_bytes(vfs[kind].at[pl.ds(0, n_layers), 0], v_send.at[4 + kind])
    wait_bytes(ts.at[pl.ds(0, n_mats), pl.ds(0, TP - 1)], v_send.at[6])
    wait_bytes(tr.at[pl.ds(0, n_mats), pl.ds(0, TP - 1)], v_send.at[7])
    wait_bytes(rp.at[pl.ds(0, n_mats), 0], v_send.at[8])
    wait_bytes(rc.at[pl.ds(0, n_mats), pl.ds(0, 3)], v_send.at[9])


def store_kernel(*refs):
    n = (len(refs) - 1) // 2
    sems = refs[-1]
    for i in range(n):
        src, dst = refs[i], refs[n + i]
        if i < 2:
            rows = src.shape[1] // STORES
            for l in range(src.shape[0]):
                for c in range(STORES):
                    pltpu.make_async_copy(src.at[l, pl.ds(c * rows, rows)], dst.at[l, pl.ds(c * rows, rows)], sems.at[i]).start()
        else:
            pltpu.make_async_copy(src, dst, sems.at[i]).start()
    for i in range(n):
        pltpu.make_async_copy(refs[i], refs[n + i], sems.at[i]).wait()


def local_step(w_in, w_out, g_in, g_out, m_in, m_out, r_in, c_in, r_out, c_out, lr, wd, b2):
    n_l, rows_in, cols_in = w_in.shape
    rows_out = w_out.shape[1]
    sw = rows_in // DP
    n_m = 2 * n_l
    vec = (cols_in + LANES + 2 * LANES - 1) // (2 * LANES) * (2 * LANES)
    hbm = pl.BlockSpec(memory_space=pltpu.HBM)
    vmem = pl.BlockSpec(memory_space=pltpu.VMEM)
    smem = pl.BlockSpec(memory_space=pltpu.SMEM)
    vm = pltpu.VMEM
    sem = pltpu.SemaphoreType.DMA
    outs = (w_in, w_out, m_in, m_out, r_in, c_in, r_out, c_out)
    res = pl.pallas_call(
        fused_kernel,
        out_shape=tuple(vm(a.shape, a.dtype) for a in outs),
        in_specs=[hbm] * 10 + [smem] * 3,
        out_specs=[vmem] * 8,
        scratch_shapes=[
            vm((n_l, 4, sw, cols_in), F32), vm((n_l, 4, rows_out, LANES), F32),
            vm((n_l, 2, 2, sw // 2, cols_in), F32), vm((n_l, 2, 2, rows_out // 2, LANES), F32),
            vm((n_l, 2, sw // 2, cols_in), F32), vm((n_l, 2, rows_out // 2, LANES), F32),
            vm((n_l, sw, cols_in), F32), vm((n_l, rows_out, LANES), F32),
            vm(r_in.shape, F32), vm(c_in.shape, F32), vm(r_out.shape, F32), vm(c_out.shape, F32),
            vm((n_l + 1, 2, 1, vec), F32), vm((n_l + 1, 2, 1, rows_out), F32),
            vm((n_l + 1, 4, 1, vec // 2), F32), vm((n_l + 1, 4, 1, rows_out // 2), F32),
            vm((n_l + 1, 2, 1, vec // 2), F32), vm((n_l + 1, 2, 1, rows_out // 2), F32),
            vm((n_m + 2, TP, 1, 2 * LANES), F32), vm((n_m + 2, TP, 1, LANES), F32),
            vm((n_m + 4, 2, 1, LANES), F32), vm((n_m + 2, 4, 1, LANES), F32),
            vm((8, LANES), F32), vm((8, LANES), F32), vm((LANES, LANES), F32),
            sem((2 + n_m,)), sem((3,)), sem((2, 2)), sem((4,)), sem((3,)), sem((2, PARTS)), sem((2 + n_m,)),
            sem((2,)), sem((n_m, 4)), sem((2,)), sem((n_m, 2)),
            sem((2,)), sem((n_m, 2)), sem((n_m, 4)), sem((2, PARTS)), sem((2,)), sem((2,)), sem((10,)), sem((n_m, 7)),
            pltpu.SemaphoreType.REGULAR((2,)),
        ],
        compiler_params=pltpu.CompilerParams(collective_id=0, has_side_effects=True, vmem_limit_bytes=34 * 2 ** 20),
        name='fused_update',
    )(g_in, g_out, w_in, w_out, m_in, m_out, r_in, c_in, r_out, c_out, lr.reshape(1), wd.reshape(1), b2.reshape(1))
    return tuple(pl.pallas_call(
        store_kernel,
        out_shape=tuple(jax.ShapeDtypeStruct(a.shape, a.dtype) for a in outs),
        in_specs=[vmem] * 8,
        out_specs=[hbm] * 8,
        scratch_shapes=[sem((8,))],
        compiler_params=pltpu.CompilerParams(vmem_limit_bytes=2 ** 20),
        name='store_out',
    )(*res))


def solution(mesh):
    in_specs = (P(None, None, 'tp'), P(None, 'tp', None), P('dp', None, None, 'tp'), P('dp', None, 'tp', None), P(None, 'dp', 'tp'), P(None, 'tp', 'dp'), P(None, 'dp'), P(None, 'tp'), P(None, 'tp'), P(None, 'dp'), P(), P(), P())
    out_specs = (P(None, None, 'tp'), P(None, 'tp', None), P(None, 'dp', 'tp'), P(None, 'tp', 'dp'), P(None, 'dp'), P(None, 'tp'), P(None, 'tp'), P(None, 'dp'))
    return jax.shard_map(local_step, mesh=mesh, in_specs=in_specs, out_specs=out_specs, check_vma=False)
```

time: 466 us -> 224 us (0.48)
  waiting for transfers between devices: 331 us -> 0 us
  Pallas kernels: 0 us -> 221 us
  blocking collectives: 82.1 us -> 0 us
  local copies, waits for them, and re-layouts: 23 us -> 0 us
  between operations: 15.8 us -> 2.58 us
  other arithmetic: 12.6 us -> 0 us
    pallas_call x0 -> x2, Pallas kernels: none -> 221 us  [the longest x1 212 us: local_step(): pl.pallas_call(fused_kernel, out_shape=tuple((vm(a.shape, a.dtype) for a...]
    reduce_scatter x2 -> x0, waiting for transfers between devices: 187 us -> none  [local_update(): lax.psum_scatter(grad_rep[0], 'dp', scatter_dimension=dp_dim, tiled=True)]
    all_gather x2 -> x0, waiting for transfers between devices: 143 us -> none  [local_update(): w_new = lax.all_gather(w_block, 'dp', axis=dp_dim, tiled=True)]
    psum x4 -> x0, blocking collectives: 82.1 us -> none  [the longest x1 39.6 us: local_update(): total_sq = lax.psum(jnp.sum(update * update, axis=(1, 2)), ('tp', 'dp'))]
    unnamed x24 -> x0, local copies, waits for them, and re-layouts: 23 us -> none
    sub x2 -> x0, other arithmetic: 7.35 us -> none  [local_update(): w_block - learn_rate * mom_new.astype(jnp.float32)]
    reduce_sum x6 -> x0, other arithmetic: 5.23 us -> none  [the longest x2 3.81 us: local_update(): col_mean = lax.psum(jnp.sum(grad_sq, axis=1), row_axis) / n_rows]
  transfers between devices with their start and end apart: 4 -> 0, of which waited for: 4 -> 0; matrix products, arithmetic and copies ran while one was open for 1% -> 0% of each run, Pallas kernels for 0% -> 0%
where the time goes in v1:
time: 224 us
  Pallas kernels  221 us (99%)
  between operations  2.58 us (1%)
    pallas_call x1, Pallas kernels, local_step(): pl.pallas_call(fused_kernel, out_shape=tuple((vm(a.shape, a.dtype) for a...  212 us
    pallas_call x1, Pallas kernels, local_step(): pl.pallas_call(store_kernel, out_shape=tuple((jax.ShapeDtypeStruct(a.shap...  8.91 us

profile of v1, /device:TPU:0, one launch (start us, length us, event | category | flops | bytes accessed | tf_op | source)
XLA Modules:
  0.0 223.7 jit_solution(7912596681567664963)
XLA Ops:
  2.6 212.2 %fused_update.1 = (f32[2,1024,1792]{2,1,0:T(8,128)S(1)}, f32[2,1280,1024]{2,1,0:T(8,128)S(1)}, bf16[2,128,1792]{2,1,0:T(8,128)(2,1)S(1)}, bf16[2,1280,128]{2,1,0...) custom-call(f32[1,2,1024,1792]{3,2,1,0:T(8,128)} %g_in.1, ...), custom_call_target="tpu_custom_call" | custom-call | tf_op jit(solution)/shard_map/fused_update/pallas_call | solution.py:507
  214.8 8.9 %store_out.1 = (f32[2,1024,1792]{2,1,0:T(8,128)}, f32[2,1280,1024]{2,1,0:T(8,128)}, bf16[2,128,1792]{2,1,0:T(8,128)(2,1)}, bf16[2,1280,128]{2,1,0:T(8,128)(2,1)}...) custom-call(f32[2,1024,1792]{2,1,0:T(8,128)S(1)} %get-tuple-element.16.refs_0_, ...), custom_call_target="tpu_custom_call" | custom-call | tf_op jit(solution)/shard_map/store_out/pallas_call | solution.py:532

commit v2 on v1

--- a/solution.py
+++ b/solution.py
@@ -9,8 +9,8 @@
 F32 = jnp.float32
 LANES = 128
 TP, DP = 4, 8
-PARTS = 4
-STORES = 4
+PARTS = 8
+STORES = 8
 
 
 def total(x):
@@ -36,7 +36,7 @@
                  ow_in, ow_out, om_in, om_out, or_in, oc_in, or_out, oc_out,
                  gm_in, gm_out, r1_in, r1_out, r2_in, r2_out, ws_in, ws_out,
                  vr_in, vc_in, vr_out, vc_out, vp_in, vp_out, vh_in, vh_out, vf_in, vf_out, ts, tr, rp, rc, short, olds, rb,
-                 ld_sem, pre_sem, st_sem, sm_sem, d2_send, d2_first, d2_recv, p1_send, p1_recv, p2_send, p2_recv,
+                 ld_sem, pre_sem, d2_send, d2_first, d2_recv, p1_send, p1_recv, p2_send, p2_recv,
                  a_send, a1_recv, a2_recv, a2_last, ad_send, ad_recv, v_send, v_recv, z_sem):
     t = lax.axis_index('tp')
     d = lax.axis_index('dp')
@@ -121,23 +121,27 @@
 
     def start_loads(m):
         mat = mats[m]
-        for i, (k, h) in enumerate(pieces):
-            sem = ld_sem.at[min(i, 2)] if m == 0 else ld_sem.at[2 + m]
-            pltpu.make_async_copy(full_view(gs, mat, 2 * k + core, h, True), half_view(gms, mat, k, h), sem).start()
-
-    def start_preload():
-        for i, (k, h) in enumerate(pieces):
+        for k, h in pieces:
+            pltpu.make_async_copy(full_view(gs, mat, 2 * k + core, h, True), half_view(gms, mat, k, h), ld_sem.at[2 + m]).start()
+
+    def load_first(lo, hi):
+        for i in range(lo, hi):
+            k, h = pieces[i]
             q = 2 * k + (1 - core)
             pltpu.make_async_copy(full_view(gs, mats[0], q, h, True), full_view(ows, mats[0], q, h, False), pre_sem.at[min(i, 2)]).start()
+            pltpu.make_async_copy(full_view(gs, mats[0], 2 * k + core, h, True), half_view(gms, mats[0], k, h), ld_sem.at[min(i, 2)]).start()
 
     def swap_first():
         views = [full_view(ows, mats[0], 2 * k + (1 - core), h, False) for k, h in pieces]
         for i in range(2):
             wait_bytes(views[i], pre_sem.at[i])
-            remote(sub(views[i], 0), sub(views[i], 0), d2_send.at[2], d2_first.at[i, 0], t, dev_c)
+            remote(sub(views[i], 0), sub(views[i], 0), d2_send.at[2], d2_first.at[0], t, dev_c)
         for p in range(1, PARTS):
             for i in range(2):
-                remote(sub(views[i], p), sub(views[i], p), d2_send.at[2], d2_first.at[i, p], t, dev_c)
+                remote(sub(views[i], p), sub(views[i], p), d2_send.at[2], d2_first.at[p], t, dev_c)
+
+    def swap_rest():
+        views = [full_view(ows, mats[0], 2 * k + (1 - core), h, False) for k, h in pieces]
         wait_bytes(gm_in.at[0, pl.ds(0, 3)], pre_sem.at[2])
         for i in range(2, 8):
             remote(views[i], views[i], d2_send.at[2], d2_recv.at[min(i - 2, 2)], t, dev_c)
@@ -160,16 +164,17 @@
         if part is not None:
             mine, other, dst = sub(mine, part), sub(other, part), sub(dst, part)
         add_into(mine, other)
-        remote(mine, dst, p1_send.at[kind], p1_recv.at[m, 2 * h + j], t, dev)
+        remote(mine, dst, p1_send.at[kind], p1_recv.at[m, j], t, dev)
 
     def stage_a_first():
         views = [chip_views(0, i)[0] for i in range(8)]
         for i in range(2):
             wait_bytes(views[i], ld_sem.at[i])
         for p in range(PARTS):
+            wait_bytes(sub(gm_in.at[0, 0], p), d2_first.at[p])
             for i in range(2):
-                wait_bytes(sub(views[i], p), d2_first.at[i, p])
                 send_first(0, i, p)
+        swap_rest()
         wait_bytes(gm_in.at[0, pl.ds(0, 3)], ld_sem.at[2])
         for i in range(2, 4):
             wait_bytes(views[i], d2_recv.at[i - 2])
@@ -190,15 +195,15 @@
 
     def stage_b(m):
         kind, l = mats[m]
+        pair = gms[kind].at[l, 0]
+        wait_bytes(pair, p1_recv.at[m, 1])
         for h, k, dev in ((0, k_y, dev_y), (1, k_x, dev_x)):
             mine = half_view(gms, mats[m], k, h)
-            wait_bytes(mine, p1_recv.at[m, 2 * h + 1])
             add_into(mine, r1s[kind].at[l, h, 1])
-            remote(mine, r2s[kind].at[l, h], p2_send.at[kind], p2_recv.at[m, h], t, dev)
+            remote(mine, r2s[kind].at[l, h], p2_send.at[kind], p2_recv.at[m], t, dev)
+        wait_bytes(pair, p1_recv.at[m, 0])
         for h in range(2):
-            mine = half_view(gms, mats[m], k_own, h)
-            wait_bytes(mine, p1_recv.at[m, 2 * h])
-            add_into(mine, r1s[kind].at[l, h, 0])
+            add_into(half_view(gms, mats[m], k_own, h), r1s[kind].at[l, h, 0])
 
     vps = (vp_in, vp_out)
     vhs = (vh_in, vh_out)
@@ -224,10 +229,9 @@
     def stage_c(m):
         kind, l = mats[m]
         mat = mats[m]
+        wait_bytes(gms[kind].at[l, 0], p2_recv.at[m])
         for h in range(2):
-            mine = half_view(gms, mat, k_own, h)
-            wait_bytes(mine, p2_recv.at[m, h])
-            add_into(mine, r2s[kind].at[l, h])
+            add_into(half_view(gms, mat, k_own, h), r2s[kind].at[l, h])
         own = vps[kind].at[l, core]
         shard = gms[kind].at[l, k_own]
         if kind == 0:
@@ -253,7 +257,7 @@
                 return acc + jnp.sum(s, axis=0, keepdims=True)
 
             short[pl.ds(m, 1), :] = lax.fori_loop(0, rows_out // LANES, body, jnp.zeros((1, LANES), F32))
-        send_core(vps[kind].at[l], v_send.at[kind], v_recv.at[m, 0])
+        send_core(vps[kind].at[l], v_send.at[0], v_recv.at[m, 0])
 
     def stage_k(m):
         kind, l = mats[m]
@@ -262,14 +266,14 @@
         size = vhs[kind].shape[3]
         half = pl.ds(pl.multiple_of(core * size, LANES), size)
         vhs[kind].at[l, chip][...] = both.at[0][:, half] + both.at[1][:, half]
-        send_chips(vhs[kind].at[l], v_send.at[2 + kind], v_recv.at[m, 1])
+        send_chips(vhs[kind].at[l], v_send.at[0], v_recv.at[m, 1])
 
     def stage_d(m):
         kind, l = mats[m]
         slots = vhs[kind].at[l]
         wait_bytes(slots.at[pl.ds(0, 3)], v_recv.at[m, 1])
         vfs[kind].at[l, core][...] = sum_slots(slots, 4)
-        send_core(vfs[kind].at[l], v_send.at[4 + kind], v_recv.at[m, 2])
+        send_core(vfs[kind].at[l], v_send.at[0], v_recv.at[m, 2])
 
     in_rows, in_cols = sw * DP, cols_in * TP
     out_rows, out_cols = rows_out * TP, sw * DP
@@ -291,7 +295,7 @@
             or_out[pl.ds(l, 1), :] = r_new
             plane = jnp.sum(r_new, axis=1, keepdims=True)
         own[:, pl.ds(LANES, LANES)] = jnp.broadcast_to(plane, (1, LANES))
-        send_tp(ts.at[m], v_send.at[6], v_recv.at[m, 3])
+        send_tp(ts.at[m], v_send.at[0], v_recv.at[m, 3])
 
     def stage_e(m):
         kind, l = mats[m]
@@ -330,22 +334,22 @@
 
             sq = lax.fori_loop(0, rows_out // LANES, body, jnp.zeros((LANES, LANES), F32))
         tr.at[m, t][...] = jnp.broadcast_to(total(sq), (1, LANES))
-        send_tp(tr.at[m], v_send.at[7], v_recv.at[m, 4])
+        send_tp(tr.at[m], v_send.at[0], v_recv.at[m, 4])
 
     def stage_f(m):
         wait_bytes(tr.at[m, pl.ds(0, TP - 1)], v_recv.at[m, 4])
         rp.at[m, core][...] = sum_slots(tr.at[m], TP)
-        send_core(rp.at[m], v_send.at[8], v_recv.at[m, 5])
+        send_core(rp.at[m], v_send.at[0], v_recv.at[m, 0])
 
     def stage_n(m):
-        wait_bytes(rp.at[m, 0], v_recv.at[m, 5])
+        wait_bytes(rp.at[m, 0], v_recv.at[m, 0])
         rc.at[m, chip][...] = rp.at[m][0] + rp.at[m][1]
-        send_chips(rc.at[m], v_send.at[9], v_recv.at[m, 6])
+        send_chips(rc.at[m], v_send.at[0], v_recv.at[m, 5])
 
     def stage_g(m):
         mat = mats[m]
         kind, l = mat
-        wait_bytes(rc.at[m, pl.ds(0, 3)], v_recv.at[m, 6])
+        wait_bytes(rc.at[m, pl.ds(0, 3)], v_recv.at[m, 5])
         size = float(in_rows * in_cols if kind == 0 else out_rows * out_cols)
         rms = jnp.sqrt(sum_slots(rc.at[m], 4) / size)
         scale = (1.0 / jnp.maximum(1.0, rms))[:, 0:1]
@@ -354,8 +358,8 @@
         old = wss[kind].at[l]
         new = full_shard(ows, mat, d)
         if l == 0:
-            wait_bytes(oms[kind], st_sem.at[kind, 0])
-            wait_bytes(wss[kind], st_sem.at[kind, 1])
+            wait_bytes(oms[kind], pre_sem.at[2 * kind])
+            wait_bytes(wss[kind], pre_sem.at[2 * kind + 1])
         step = 16 if kind == 0 else 128
 
         def body(i, carry):
@@ -370,10 +374,10 @@
         q = d
         a = full_view(ows, mat, q, 0, False)
         b = full_view(ows, mat, q, 1, False)
-        remote(a, a, a_send.at[kind], a1_recv.at[m, 0], t, dev_y)
-        remote(b, b, a_send.at[kind], a1_recv.at[m, 1], t, dev_x)
+        remote(a, a, a_send.at[kind], a1_recv.at[m], t, dev_y)
+        remote(b, b, a_send.at[kind], a1_recv.at[m], t, dev_x)
         remote(a, a, a_send.at[kind], a2_recv.at[m, 0], t, dev_x)
-        remote(b, b, a_send.at[kind], a2_recv.at[m, 1], t, dev_y)
+        remote(b, b, a_send.at[kind], a2_recv.at[m, 0], t, dev_y)
         pass_core(m, new)
 
     def pass_core(m, view):
@@ -385,78 +389,88 @@
         kind = mat[0]
         a = full_view(ows, mat, 2 * k_y + core, 0, False)
         b = full_view(ows, mat, 2 * k_x + core, 1, False)
-        for i, (view, dev) in enumerate(((a, dev_x), (b, dev_y))):
-            wait_bytes(view, a1_recv.at[m, i])
+        wait_bytes(gms[kind].at[mat[1], 0], a1_recv.at[m])
+        for view, dev in ((a, dev_x), (b, dev_y)):
             if m < n_mats - 1:
-                remote(view, view, a_send.at[kind], a2_recv.at[m, 2 + i], t, dev)
+                remote(view, view, a_send.at[kind], a2_recv.at[m, 1], t, dev)
             else:
                 for p in range(PARTS):
-                    remote(sub(view, p), sub(view, p), a_send.at[kind], a2_last.at[i, p], t, dev)
+                    remote(sub(view, p), sub(view, p), a_send.at[kind], a2_last.at[p], t, dev)
         pass_core(m, a)
         pass_core(m, b)
 
     def stage_i(m):
-        last = m == n_mats - 1
-        for i, k, h in ((0, k_x, 0), (1, k_y, 1)):
-            view = full_view(ows, mats[m], 2 * k + core, h, False)
-            wait_bytes(view, a2_recv.at[m, i])
-            pass_core(m, view)
+        kind, l = mats[m]
+        pair = gms[kind].at[l, 0]
+        wait_bytes(pair, a2_recv.at[m, 0])
+        pass_core(m, full_view(ows, mats[m], 2 * k_x + core, 0, False))
+        pass_core(m, full_view(ows, mats[m], 2 * k_y + core, 1, False))
         views = [full_view(ows, mats[m], 2 * k_d + core, h, False) for h in range(2)]
-        if not last:
-            for i in range(2):
-                wait_bytes(views[i], a2_recv.at[m, 2 + i])
-                pass_core(m, views[i])
+        if m < n_mats - 1:
+            wait_bytes(pair, a2_recv.at[m, 1])
+            for view in views:
+                pass_core(m, view)
         else:
             for p in range(PARTS):
-                for i in range(2):
-                    wait_bytes(sub(views[i], p), a2_last.at[i, p])
-                    pass_core(m, sub(views[i], p))
+                wait_bytes(sub(pair, p), a2_last.at[p])
+                for view in views:
+                    pass_core(m, sub(view, p))
 
     small = [(r_in, vr_in), (c_in, vc_in), (r_out, vr_out), (c_out, vc_out)]
     barrier = pltpu.get_barrier_semaphore()
-    z_near = jnp.minimum(t, 1) + jnp.minimum(TP - 1 - t, 1)
-
-    def signal_z(sem):
+    z_low = jnp.minimum(t, 1)
+    z_high = jnp.minimum(TP - 1 - t, 1)
+
+    def signal_low(sem):
         @pl.when(t > 0)
         def _():
             pl.semaphore_signal(sem, inc=1, device_id=(t - 1, d), device_id_type=MESH)
 
+    def signal_high(sem):
         @pl.when(t < TP - 1)
         def _():
             pl.semaphore_signal(sem, inc=1, device_id=(t + 1, d), device_id_type=MESH)
 
     for dev in (dev_x, dev_y, dev_c):
         pl.semaphore_signal(barrier, inc=1, device_id=(t, dev), device_id_type=MESH)
-    signal_z(barrier)
-    start_preload()
-    start_loads(0)
-    pl.semaphore_wait(barrier, 3 + z_near)
+    signal_high(barrier)
+    load_first(0, 2)
+    load_first(2, 8)
+    pl.semaphore_wait(barrier, 3 + z_low)
     swap_first()
     stage_a_first()
     start_loads(1)
     start_swap(1)
-    signal_z(z_sem.at[0])
+    signal_low(z_sem.at[0])
     wait_bytes(gm_in.at[0, pl.ds(0, 2)], d2_recv.at[2])
     keep_first(0)
     stage_a(1)
     for i, (src, dst) in enumerate(small):
-        pltpu.make_async_copy(src, dst, sm_sem.at[i]).start()
+        pltpu.make_async_copy(src, dst, ld_sem.at[i]).start()
     for m, (kind, l) in enumerate(mats):
-        pltpu.make_async_copy((m_in, m_out)[kind].at[l], oms[kind].at[l], st_sem.at[kind, 0]).start()
+        pltpu.make_async_copy((m_in, m_out)[kind].at[l], oms[kind].at[l], pre_sem.at[2 * kind]).start()
         src = w_in.at[l, pl.ds(pl.multiple_of(d * sw, sw), sw), :] if kind == 0 else w_out.at[l, :, pl.ds(pl.multiple_of(d * LANES, LANES), LANES)]
-        pltpu.make_async_copy(src, wss[kind].at[l], st_sem.at[kind, 1]).start()
+        pltpu.make_async_copy(src, wss[kind].at[l], pre_sem.at[2 * kind + 1]).start()
     wait_bytes(gm_in.at[0], d2_send.at[2])
-    pl.semaphore_wait(z_sem.at[0], z_near)
-    signal_z(z_sem.at[1])
+
+    @pl.when(t < TP - 1)
+    def _():
+        pl.semaphore_wait(z_sem.at[0], 1)
+
+    signal_low(z_sem.at[1])
+    signal_high(z_sem.at[1])
     for i, (src, dst) in enumerate(small):
-        wait_bytes(dst, sm_sem.at[i])
+        wait_bytes(dst, ld_sem.at[i])
     order = 's2 b0 a2 s3 b1 c0 k0 a3 b2 c1 k1 d0 l0 e0 f0 n0 b3 c2 k2 g0 d1 l1 e1 f1 n1 c3 k3 d2 l2 h0 e2 f2 n2 g1 i0 d3 l3 e3 f3 n3 h1 g2 i1 h2 g3 i2 h3 i3'
     def stage_s(m):
         start_loads(m)
         start_swap(m)
 
     stages = dict(s=stage_s, a=stage_a, b=stage_b, c=stage_c, d=stage_d, e=stage_e, f=stage_f, g=stage_g, h=stage_h, i=stage_i, k=stage_k, l=stage_l, n=stage_n)
-    pl.semaphore_wait(z_sem.at[1], z_near)
+    pl.semaphore_wait(z_sem.at[1], z_low + z_high)
+    signal_low(z_sem.at[2])
+    signal_high(z_sem.at[2])
+    pl.semaphore_wait(z_sem.at[2], z_low + z_high)
     for item in order.split():
         stages[item[0]](int(item[1]))
     for kind in range(2):
@@ -467,13 +481,9 @@
         wait_bytes(r2s[kind], p2_send.at[kind])
         wait_bytes(gm.at[:, pl.ds(0, 3)], a_send.at[kind])
         wait_bytes(gm, ad_send.at[kind])
-        wait_bytes(vps[kind].at[pl.ds(0, n_layers), 0], v_send.at[kind])
-        wait_bytes(vhs[kind].at[pl.ds(0, n_layers), pl.ds(0, 3)], v_send.at[2 + kind])
-        wait_bytes(vfs[kind].at[pl.ds(0, n_layers), 0], v_send.at[4 + kind])
-    wait_bytes(ts.at[pl.ds(0, n_mats), pl.ds(0, TP - 1)], v_send.at[6])
-    wait_bytes(tr.at[pl.ds(0, n_mats), pl.ds(0, TP - 1)], v_send.at[7])
-    wait_bytes(rp.at[pl.ds(0, n_mats), 0], v_send.at[8])
-    wait_bytes(rc.at[pl.ds(0, n_mats), pl.ds(0, 3)], v_send.at[9])
+    sizes = [n_layers * (vps[k].shape[3] + (3 + 1) * vhs[k].shape[3]) for k in range(2)]
+    sent = sum(sizes) + n_mats * ((TP - 1) * 3 + 1 + 3) * LANES
+    wait_bytes(gm_out.at[0, 0, pl.ds(0, sent // LANES)], v_send.at[0])
 
 
 def store_kernel(*refs):
@@ -521,10 +531,10 @@
             vm((n_m + 2, TP, 1, 2 * LANES), F32), vm((n_m + 2, TP, 1, LANES), F32),
             vm((n_m + 4, 2, 1, LANES), F32), vm((n_m + 2, 4, 1, LANES), F32),
             vm((8, LANES), F32), vm((8, LANES), F32), vm((LANES, LANES), F32),
-            sem((2 + n_m,)), sem((3,)), sem((2, 2)), sem((4,)), sem((3,)), sem((2, PARTS)), sem((2 + n_m,)),
-            sem((2,)), sem((n_m, 4)), sem((2,)), sem((n_m, 2)),
-            sem((2,)), sem((n_m, 2)), sem((n_m, 4)), sem((2, PARTS)), sem((2,)), sem((2,)), sem((10,)), sem((n_m, 7)),
-            pltpu.SemaphoreType.REGULAR((2,)),
+            sem((2 + n_m,)), sem((4,)), sem((3,)), sem((PARTS,)), sem((2 + n_m,)),
+            sem((2,)), sem((n_m, 2)), sem((2,)), sem((n_m,)),
+            sem((2,)), sem((n_m,)), sem((n_m, 2)), sem((PARTS,)), sem((2,)), sem((2,)), sem((1,)), sem((n_m, 6)),
+            pltpu.SemaphoreType.REGULAR((3,)),
         ],
         compiler_params=pltpu.CompilerParams(collective_id=0, has_side_effects=True, vmem_limit_bytes=34 * 2 ** 20),
         name='fused_update',

time: 224 us -> 223 us (level)
  no operation moved by 1% of the time
where the time goes in v2:
time: 223 us
  Pallas kernels  220 us (99%)
  between operations  2.58 us (1%)
    pallas_call x1, Pallas kernels, local_step(): pl.pallas_call(fused_kernel, out_shape=tuple((vm(a.shape, a.dtype) for a...  211 us
    pallas_call x1, Pallas kernels, local_step(): pl.pallas_call(store_kernel, out_shape=tuple((jax.ShapeDtypeStruct(a.shap...  8.89 us

profile of v2, /device:TPU:0, one launch (start us, length us, event | category | flops | bytes accessed | tf_op | source)
XLA Modules:
  0.0 222.6 jit_solution(12378851671056399969)
XLA Ops:
  2.6 211.1 %fused_update.1 = (f32[2,1024,1792]{2,1,0:T(8,128)S(1)}, f32[2,1280,1024]{2,1,0:T(8,128)S(1)}, bf16[2,128,1792]{2,1,0:T(8,128)(2,1)S(1)}, bf16[2,1280,128]{2,1,0...) custom-call(f32[1,2,1024,1792]{3,2,1,0:T(8,128)} %g_in.1, ...), custom_call_target="tpu_custom_call" | custom-call | tf_op jit(solution)/shard_map/fused_update/pallas_call | solution.py:517
  213.7 8.9 %store_out.1 = (f32[2,1024,1792]{2,1,0:T(8,128)}, f32[2,1280,1024]{2,1,0:T(8,128)}, bf16[2,128,1792]{2,1,0:T(8,128)(2,1)}, bf16[2,1280,128]{2,1,0:T(8,128)(2,1)}...) custom-call(f32[2,1024,1792]{2,1,0:T(8,128)S(1)} %get-tuple-element.16.refs_0_, ...), custom_call_target="tpu_custom_call" | custom-call | tf_op jit(solution)/shard_map/store_out/pallas_call | solution.py:542

commit v3 on v2

--- a/solution.py
+++ b/solution.py
@@ -37,7 +37,7 @@
                  gm_in, gm_out, r1_in, r1_out, r2_in, r2_out, ws_in, ws_out,
                  vr_in, vc_in, vr_out, vc_out, vp_in, vp_out, vh_in, vh_out, vf_in, vf_out, ts, tr, rp, rc, short, olds, rb,
                  ld_sem, pre_sem, d2_send, d2_first, d2_recv, p1_send, p1_recv, p2_send, p2_recv,
-                 a_send, a1_recv, a2_recv, a2_last, ad_send, ad_recv, v_send, v_recv, z_sem):
+                 a_send, a2_last, ad_send, v_send, v_recv, z_sem):
     t = lax.axis_index('tp')
     d = lax.axis_index('dp')
     core = lax.rem(d, 2)
@@ -257,23 +257,23 @@
                 return acc + jnp.sum(s, axis=0, keepdims=True)
 
             short[pl.ds(m, 1), :] = lax.fori_loop(0, rows_out // LANES, body, jnp.zeros((1, LANES), F32))
-        send_core(vps[kind].at[l], v_send.at[0], v_recv.at[m, 0])
+        send_core(vps[kind].at[l], v_send.at[0], v_recv.at[3 + m])
 
     def stage_k(m):
         kind, l = mats[m]
         both = vps[kind].at[l]
-        wait_bytes(both.at[0], v_recv.at[m, 0])
+        wait_bytes(both.at[0], v_recv.at[3 + m])
         size = vhs[kind].shape[3]
         half = pl.ds(pl.multiple_of(core * size, LANES), size)
         vhs[kind].at[l, chip][...] = both.at[0][:, half] + both.at[1][:, half]
-        send_chips(vhs[kind].at[l], v_send.at[0], v_recv.at[m, 1])
+        send_chips(vhs[kind].at[l], v_send.at[0], v_recv.at[3 + n_mats + m])
 
     def stage_d(m):
         kind, l = mats[m]
         slots = vhs[kind].at[l]
-        wait_bytes(slots.at[pl.ds(0, 3)], v_recv.at[m, 1])
+        wait_bytes(slots.at[pl.ds(0, 3)], v_recv.at[3 + n_mats + m])
         vfs[kind].at[l, core][...] = sum_slots(slots, 4)
-        send_core(vfs[kind].at[l], v_send.at[0], v_recv.at[m, 2])
+        send_core(vfs[kind].at[l], v_send.at[0], v_recv.at[0])
 
     in_rows, in_cols = sw * DP, cols_in * TP
     out_rows, out_cols = rows_out * TP, sw * DP
@@ -281,25 +281,25 @@
     def stage_l(m):
         kind, l = mats[m]
         both = vfs[kind].at[l]
-        wait_bytes(both.at[0], v_recv.at[m, 2])
+        wait_bytes(both.at[0], v_recv.at[0])
         acc = jnp.concatenate([both[0], both[1]], axis=1)
         own = ts.at[m, t]
         own[:, pl.ds(0, LANES)] = short[pl.ds(m, 1), :]
         if kind == 0:
             col_sum = acc[:, :cols_in]
             oc_in[pl.ds(l, 1), :] = b2 * vc_in[pl.ds(l, 1), :] + (1.0 - b2) * (col_sum / in_rows)
-            plane = jnp.sum(col_sum, axis=1, keepdims=True)
+            plane = jnp.sum(col_sum / in_rows, axis=1, keepdims=True)
             olds[pl.ds(l, 1), :] = acc[:, cols_in:cols_in + LANES]
         else:
             r_new = b2 * vr_out[pl.ds(l, 1), :] + (1.0 - b2) * (acc / out_cols)
             or_out[pl.ds(l, 1), :] = r_new
             plane = jnp.sum(r_new, axis=1, keepdims=True)
         own[:, pl.ds(LANES, LANES)] = jnp.broadcast_to(plane, (1, LANES))
-        send_tp(ts.at[m], v_send.at[0], v_recv.at[m, 3])
+        send_tp(ts.at[m], v_send.at[0], v_recv.at[1])
 
     def stage_e(m):
         kind, l = mats[m]
-        wait_bytes(ts.at[m, pl.ds(0, TP - 1)], v_recv.at[m, 3])
+        wait_bytes(ts.at[m, pl.ds(0, TP - 1)], v_recv.at[1])
         acc = sum_slots(ts.at[m], TP)
         vec = acc[:, :LANES]
         tot = acc[:, LANES:LANES + 1]
@@ -308,7 +308,7 @@
             r_new = b2 * vr_in[pl.ds(l, 1), :] + (1.0 - b2) * (vec / in_cols)
             or_in[pl.ds(l, 1), :] = r_new
             old = jnp.sum(olds[pl.ds(l, 1), :], axis=1, keepdims=True)
-            avg = (b2 * old + (1.0 - b2) * (tot / in_cols)) / in_rows
+            avg = b2 * (old / in_rows) + (1.0 - b2) * (tot / in_cols)
             rb[pl.ds(0, LANES), :] = to_rows(1.0 / jnp.sqrt(r_new))
             cj = jnp.sqrt(avg) / jnp.sqrt(oc_in[pl.ds(l, 1), :])
 
@@ -334,22 +334,22 @@
 
             sq = lax.fori_loop(0, rows_out // LANES, body, jnp.zeros((LANES, LANES), F32))
         tr.at[m, t][...] = jnp.broadcast_to(total(sq), (1, LANES))
-        send_tp(tr.at[m], v_send.at[0], v_recv.at[m, 4])
+        send_tp(tr.at[m], v_send.at[0], v_recv.at[2])
 
     def stage_f(m):
-        wait_bytes(tr.at[m, pl.ds(0, TP - 1)], v_recv.at[m, 4])
+        wait_bytes(tr.at[m, pl.ds(0, TP - 1)], v_recv.at[2])
         rp.at[m, core][...] = sum_slots(tr.at[m], TP)
-        send_core(rp.at[m], v_send.at[0], v_recv.at[m, 0])
+        send_core(rp.at[m], v_send.at[0], v_recv.at[3 + m])
 
     def stage_n(m):
-        wait_bytes(rp.at[m, 0], v_recv.at[m, 0])
+        wait_bytes(rp.at[m, 0], v_recv.at[3 + m])
         rc.at[m, chip][...] = rp.at[m][0] + rp.at[m][1]
-        send_chips(rc.at[m], v_send.at[0], v_recv.at[m, 5])
+        send_chips(rc.at[m], v_send.at[0], v_recv.at[3 + 2 * n_mats + m])
 
     def stage_g(m):
         mat = mats[m]
         kind, l = mat
-        wait_bytes(rc.at[m, pl.ds(0, 3)], v_recv.at[m, 5])
+        wait_bytes(rc.at[m, pl.ds(0, 3)], v_recv.at[3 + 2 * n_mats + m])
         size = float(in_rows * in_cols if kind == 0 else out_rows * out_cols)
         rms = jnp.sqrt(sum_slots(rc.at[m], 4) / size)
         scale = (1.0 / jnp.maximum(1.0, rms))[:, 0:1]
@@ -374,25 +374,25 @@
         q = d
         a = full_view(ows, mat, q, 0, False)
         b = full_view(ows, mat, q, 1, False)
-        remote(a, a, a_send.at[kind], a1_recv.at[m], t, dev_y)
-        remote(b, b, a_send.at[kind], a1_recv.at[m], t, dev_x)
-        remote(a, a, a_send.at[kind], a2_recv.at[m, 0], t, dev_x)
-        remote(b, b, a_send.at[kind], a2_recv.at[m, 0], t, dev_y)
+        remote(a, a, a_send.at[kind], p2_recv.at[m], t, dev_y)
+        remote(b, b, a_send.at[kind], p2_recv.at[m], t, dev_x)
+        remote(a, a, a_send.at[kind], p1_recv.at[m, 0], t, dev_x)
+        remote(b, b, a_send.at[kind], p1_recv.at[m, 0], t, dev_y)
         pass_core(m, new)
 
     def pass_core(m, view):
         kind = mats[m][0]
-        remote(view, view, ad_send.at[kind], ad_recv.at[kind], t, dev_c)
+        remote(view, view, ad_send.at[kind], d2_recv.at[kind], t, dev_c)
 
     def stage_h(m):
         mat = mats[m]
         kind = mat[0]
         a = full_view(ows, mat, 2 * k_y + core, 0, False)
         b = full_view(ows, mat, 2 * k_x + core, 1, False)
-        wait_bytes(gms[kind].at[mat[1], 0], a1_recv.at[m])
+        wait_bytes(gms[kind].at[mat[1], 0], p2_recv.at[m])
         for view, dev in ((a, dev_x), (b, dev_y)):
             if m < n_mats - 1:
-                remote(view, view, a_send.at[kind], a2_recv.at[m, 1], t, dev)
+                remote(view, view, a_send.at[kind], p1_recv.at[m, 1], t, dev)
             else:
                 for p in range(PARTS):
                     remote(sub(view, p), sub(view, p), a_send.at[kind], a2_last.at[p], t, dev)
@@ -402,12 +402,12 @@
     def stage_i(m):
         kind, l = mats[m]
         pair = gms[kind].at[l, 0]
-        wait_bytes(pair, a2_recv.at[m, 0])
+        wait_bytes(pair, p1_recv.at[m, 0])
         pass_core(m, full_view(ows, mats[m], 2 * k_x + core, 0, False))
         pass_core(m, full_view(ows, mats[m], 2 * k_y + core, 1, False))
         views = [full_view(ows, mats[m], 2 * k_d + core, h, False) for h in range(2)]
         if m < n_mats - 1:
-            wait_bytes(pair, a2_recv.at[m, 1])
+            wait_bytes(pair, p1_recv.at[m, 1])
             for view in views:
                 pass_core(m, view)
         else:
@@ -475,7 +475,7 @@
         stages[item[0]](int(item[1]))
     for kind in range(2):
         gm = gms[kind]
-        wait_bytes(gm, ad_recv.at[kind])
+        wait_bytes(gm, d2_recv.at[kind])
         wait_bytes(gm.at[pl.ds(0, n_layers - 1 + kind)], d2_send.at[kind])
         wait_bytes(r1s[kind], p1_send.at[kind])
         wait_bytes(r2s[kind], p2_send.at[kind])
@@ -533,7 +533,7 @@
             vm((8, LANES), F32), vm((8, LANES), F32), vm((LANES, LANES), F32),
             sem((2 + n_m,)), sem((4,)), sem((3,)), sem((PARTS,)), sem((2 + n_m,)),
             sem((2,)), sem((n_m, 2)), sem((2,)), sem((n_m,)),
-            sem((2,)), sem((n_m,)), sem((n_m, 2)), sem((PARTS,)), sem((2,)), sem((2,)), sem((1,)), sem((n_m, 6)),
+            sem((2,)), sem((PARTS,)), sem((2,)), sem((1,)), sem((3 + 3 * n_m,)),
             pltpu.SemaphoreType.REGULAR((3,)),
         ],
         compiler_params=pltpu.CompilerParams(collective_id=0, has_side_effects=True, vmem_limit_bytes=34 * 2 ** 20),

time: 223 us -> 223 us (level)
  no operation moved by 1% of the time
where the time goes in v3:
time: 223 us; the launch traced here: 222 us
  Pallas kernels  220 us (99%)
  between operations  2.58 us (1%)
    pallas_call x1, Pallas kernels, local_step(): pl.pallas_call(fused_kernel, out_shape=tuple((vm(a.shape, a.dtype) for a...  211 us
    pallas_call x1, Pallas kernels, local_step(): pl.pallas_call(store_kernel, out_shape=tuple((jax.ShapeDtypeStruct(a.shap...  8.89 us

profile of v3, /device:TPU:0, one launch (start us, length us, event | category | flops | bytes accessed | tf_op | source)
XLA Modules:
  0.0 222.4 jit_solution(4812867718955370999)
XLA Ops:
  2.6 210.9 %fused_update.1 = (f32[2,1024,1792]{2,1,0:T(8,128)S(1)}, f32[2,1280,1024]{2,1,0:T(8,128)S(1)}, bf16[2,128,1792]{2,1,0:T(8,128)(2,1)S(1)}, bf16[2,1280,128]{2,1,0...) custom-call(f32[1,2,1024,1792]{3,2,1,0:T(8,128)} %g_in.1, ...), custom_call_target="tpu_custom_call" | custom-call | tf_op jit(solution)/shard_map/fused_update/pallas_call | solution.py:517
  213.5 8.9 %store_out.1 = (f32[2,1024,1792]{2,1,0:T(8,128)}, f32[2,1280,1024]{2,1,0:T(8,128)}, bf16[2,128,1792]{2,1,0:T(8,128)(2,1)}, bf16[2,1280,128]{2,1,0:T(8,128)(2,1)}...) custom-call(f32[2,1024,1792]{2,1,0:T(8,128)S(1)} %get-tuple-element.16.refs_0_, ...), custom_call_target="tpu_custom_call" | custom-call | tf_op jit(solution)/shard_map/store_out/pallas_call | solution.py:542

commit v4 on v3

--- a/solution.py
+++ b/solution.py
@@ -9,7 +9,9 @@
 F32 = jnp.float32
 LANES = 128
 TP, DP = 4, 8
-PARTS = 8
+FIRST = (1, 1, 2, 4)
+LAST = (4, 2, 1, 1)
+PARTS = 4
 STORES = 8
 
 
@@ -60,6 +62,7 @@
     n_mats = len(mats)
     sw = gm_in.shape[2]
     half_in = sw // 2
+    first = half_in * FIRST[0] // sum(FIRST)
     cols_in = gm_in.shape[3]
     rows_out = gm_out.shape[2]
     half_out = rows_out // 2
@@ -115,28 +118,40 @@
     pieces = [(k_d, 0), (k_d, 1), (k_x, 0), (k_y, 1), (k_y, 0), (k_x, 1), (k_own, 0), (k_own, 1)]
     routes = [(0, 1, dev_x), (1, 1, dev_y), (0, 0, dev_x), (1, 0, dev_y)]
 
-    def sub(ref, i):
-        rows = ref.shape[0] // PARTS
-        return ref.at[pl.ds(i * rows, rows)]
+    def sub(ref, i, plan=FIRST):
+        unit = ref.shape[0] // sum(plan)
+        return ref.at[pl.ds(sum(plan[:i]) * unit, plan[i] * unit)]
 
     def start_loads(m):
         mat = mats[m]
         for k, h in pieces:
             pltpu.make_async_copy(full_view(gs, mat, 2 * k + core, h, True), half_view(gms, mat, k, h), ld_sem.at[2 + m]).start()
 
-    def load_first(lo, hi):
-        for i in range(lo, hi):
+    def load_first():
+        def views(i):
             k, h = pieces[i]
-            q = 2 * k + (1 - core)
-            pltpu.make_async_copy(full_view(gs, mats[0], q, h, True), full_view(ows, mats[0], q, h, False), pre_sem.at[min(i, 2)]).start()
-            pltpu.make_async_copy(full_view(gs, mats[0], 2 * k + core, h, True), half_view(gms, mats[0], k, h), ld_sem.at[min(i, 2)]).start()
+            q, mine = 2 * k + (1 - core), 2 * k + core
+            return ((full_view(gs, mats[0], q, h, True), full_view(ows, mats[0], q, h, False), pre_sem),
+                    (full_view(gs, mats[0], mine, h, True), half_view(gms, mats[0], k, h), ld_sem))
+
+        for step in range(2):
+            for which in range(2):
+                for i in range(2):
+                    src, dst, sem = views(i)[which]
+                    rows = pl.ds(0, first) if step == 0 else pl.ds(first, half_in - first)
+                    pltpu.make_async_copy(src.at[rows], dst.at[rows], sem.at[step]).start()
+        for i in range(2, 8):
+            for src, dst, sem in views(i):
+                pltpu.make_async_copy(src, dst, sem.at[2]).start()
+
+    def first_bytes(step):
+        return gm_in.at[0, 0, pl.ds(0, 2 * first if step == 0 else 2 * (half_in - first))]
 
     def swap_first():
         views = [full_view(ows, mats[0], 2 * k + (1 - core), h, False) for k, h in pieces]
-        for i in range(2):
-            wait_bytes(views[i], pre_sem.at[i])
-            remote(sub(views[i], 0), sub(views[i], 0), d2_send.at[2], d2_first.at[0], t, dev_c)
-        for p in range(1, PARTS):
+        for p in range(PARTS):
+            if p < 2:
+                wait_bytes(first_bytes(p), pre_sem.at[p])
             for i in range(2):
                 remote(sub(views[i], p), sub(views[i], p), d2_send.at[2], d2_first.at[p], t, dev_c)
 
@@ -168,9 +183,9 @@
 
     def stage_a_first():
         views = [chip_views(0, i)[0] for i in range(8)]
-        for i in range(2):
-            wait_bytes(views[i], ld_sem.at[i])
         for p in range(PARTS):
+            if p < 2:
+                wait_bytes(first_bytes(p), ld_sem.at[p])
             wait_bytes(sub(gm_in.at[0, 0], p), d2_first.at[p])
             for i in range(2):
                 send_first(0, i, p)
@@ -395,7 +410,8 @@
                 remote(view, view, a_send.at[kind], p1_recv.at[m, 1], t, dev)
             else:
                 for p in range(PARTS):
-                    remote(sub(view, p), sub(view, p), a_send.at[kind], a2_last.at[p], t, dev)
+                    part = sub(view, p, LAST)
+                    remote(part, part, a_send.at[kind], a2_last.at[p], t, dev)
         pass_core(m, a)
         pass_core(m, b)
 
@@ -412,9 +428,9 @@
                 pass_core(m, view)
         else:
             for p in range(PARTS):
-                wait_bytes(sub(pair, p), a2_last.at[p])
+                wait_bytes(sub(pair, p, LAST), a2_last.at[p])
                 for view in views:
-                    pass_core(m, sub(view, p))
+                    pass_core(m, sub(view, p, LAST))
 
     small = [(r_in, vr_in), (c_in, vc_in), (r_out, vr_out), (c_out, vc_out)]
     barrier = pltpu.get_barrier_semaphore()
@@ -434,8 +450,7 @@
     for dev in (dev_x, dev_y, dev_c):
         pl.semaphore_signal(barrier, inc=1, device_id=(t, dev), device_id_type=MESH)
     signal_high(barrier)
-    load_first(0, 2)
-    load_first(2, 8)
+    load_first()
     pl.semaphore_wait(barrier, 3 + z_low)
     swap_first()
     stage_a_first()

time: 223 us -> 222 us (level)
  no operation moved by 1% of the time
where the time goes in v4:
time: 222 us
  Pallas kernels  220 us (99%)
  between operations  2.58 us (1%)
    pallas_call x1, Pallas kernels, local_step(): pl.pallas_call(fused_kernel, out_shape=tuple((vm(a.shape, a.dtype) for a...  211 us
    pallas_call x1, Pallas kernels, local_step(): pl.pallas_call(store_kernel, out_shape=tuple((jax.ShapeDtypeStruct(a.shap...  8.89 us

profile of v4, /device:TPU:0, one launch (start us, length us, event | category | flops | bytes accessed | tf_op | source)
XLA Modules:
  0.0 222.2 jit_solution(6636475515746297445)
XLA Ops:
  2.6 210.8 %fused_update.1 = (f32[2,1024,1792]{2,1,0:T(8,128)S(1)}, f32[2,1280,1024]{2,1,0:T(8,128)S(1)}, bf16[2,128,1792]{2,1,0:T(8,128)(2,1)S(1)}, bf16[2,1280,128]{2,1,0...) custom-call(f32[1,2,1024,1792]{3,2,1,0:T(8,128)} %g_in.1, ...), custom_call_target="tpu_custom_call" | custom-call | tf_op jit(solution)/shard_map/fused_update/pallas_call | solution.py:532
  213.4 8.9 %store_out.1 = (f32[2,1024,1792]{2,1,0:T(8,128)}, f32[2,1280,1024]{2,1,0:T(8,128)}, bf16[2,128,1792]{2,1,0:T(8,128)(2,1)}, bf16[2,1280,128]{2,1,0:T(8,128)(2,1)}...) custom-call(f32[2,1024,1792]{2,1,0:T(8,128)S(1)} %get-tuple-element.16.refs_0_, ...), custom_call_target="tpu_custom_call" | custom-call | tf_op jit(solution)/shard_map/store_out/pallas_call | solution.py:557

commit v5 on v4

--- a/solution.py
+++ b/solution.py
@@ -39,7 +39,7 @@
                  gm_in, gm_out, r1_in, r1_out, r2_in, r2_out, ws_in, ws_out,
                  vr_in, vc_in, vr_out, vc_out, vp_in, vp_out, vh_in, vh_out, vf_in, vf_out, ts, tr, rp, rc, short, olds, rb,
                  ld_sem, pre_sem, d2_send, d2_first, d2_recv, p1_send, p1_recv, p2_send, p2_recv,
-                 a_send, a2_last, ad_send, v_send, v_recv, z_sem):
+                 a2_last, v_send, v_recv, z_sem):
     t = lax.axis_index('tp')
     d = lax.axis_index('dp')
     core = lax.rem(d, 2)
@@ -125,7 +125,7 @@
     def start_loads(m):
         mat = mats[m]
         for k, h in pieces:
-            pltpu.make_async_copy(full_view(gs, mat, 2 * k + core, h, True), half_view(gms, mat, k, h), ld_sem.at[2 + m]).start()
+            pltpu.make_async_copy(full_view(gs, mat, 2 * k + core, h, True), half_view(gms, mat, k, h), ld_sem.at[3]).start()
 
     def load_first():
         def views(i):
@@ -202,7 +202,7 @@
     def stage_a(m):
         kind, l = mats[m]
         gm = gms[kind].at[l]
-        wait_bytes(gm, ld_sem.at[2 + m])
+        wait_bytes(gm, ld_sem.at[3])
         wait_bytes(gm, d2_recv.at[2 + m])
         for i in range(4):
             send_first(m, i)
@@ -373,6 +373,8 @@
         old = wss[kind].at[l]
         new = full_shard(ows, mat, d)
         if l == 0:
+            wait_bytes(r1s[kind], p1_send.at[kind])
+            wait_bytes(gms[kind].at[pl.ds(0, n_layers - 1 + kind)], d2_send.at[kind])
             wait_bytes(oms[kind], pre_sem.at[2 * kind])
             wait_bytes(wss[kind], pre_sem.at[2 * kind + 1])
         step = 16 if kind == 0 else 128
@@ -389,15 +391,15 @@
         q = d
         a = full_view(ows, mat, q, 0, False)
         b = full_view(ows, mat, q, 1, False)
-        remote(a, a, a_send.at[kind], p2_recv.at[m], t, dev_y)
-        remote(b, b, a_send.at[kind], p2_recv.at[m], t, dev_x)
-        remote(a, a, a_send.at[kind], p1_recv.at[m, 0], t, dev_x)
-        remote(b, b, a_send.at[kind], p1_recv.at[m, 0], t, dev_y)
+        remote(a, a, p1_send.at[kind], p2_recv.at[m], t, dev_y)
+        remote(b, b, p1_send.at[kind], p2_recv.at[m], t, dev_x)
+        remote(a, a, p1_send.at[kind], p1_recv.at[m, 0], t, dev_x)
+        remote(b, b, p1_send.at[kind], p1_recv.at[m, 0], t, dev_y)
         pass_core(m, new)
 
     def pass_core(m, view):
         kind = mats[m][0]
-        remote(view, view, ad_send.at[kind], d2_recv.at[kind], t, dev_c)
+        remote(view, view, d2_send.at[kind], d2_recv.at[kind], t, dev_c)
 
     def stage_h(m):
         mat = mats[m]
@@ -407,11 +409,11 @@
         wait_bytes(gms[kind].at[mat[1], 0], p2_recv.at[m])
         for view, dev in ((a, dev_x), (b, dev_y)):
             if m < n_mats - 1:
-                remote(view, view, a_send.at[kind], p1_recv.at[m, 1], t, dev)
+                remote(view, view, p1_send.at[kind], p1_recv.at[m, 1], t, dev)
             else:
                 for p in range(PARTS):
                     part = sub(view, p, LAST)
-                    remote(part, part, a_send.at[kind], a2_last.at[p], t, dev)
+                    remote(part, part, p1_send.at[kind], a2_last.at[p], t, dev)
         pass_core(m, a)
         pass_core(m, b)
 
@@ -491,11 +493,9 @@
     for kind in range(2):
         gm = gms[kind]
         wait_bytes(gm, d2_recv.at[kind])
-        wait_bytes(gm.at[pl.ds(0, n_layers - 1 + kind)], d2_send.at[kind])
-        wait_bytes(r1s[kind], p1_send.at[kind])
         wait_bytes(r2s[kind], p2_send.at[kind])
-        wait_bytes(gm.at[:, pl.ds(0, 3)], a_send.at[kind])
-        wait_bytes(gm, ad_send.at[kind])
+        wait_bytes(gm.at[:, pl.ds(0, 3)], p1_send.at[kind])
+        wait_bytes(gm, d2_send.at[kind])
     sizes = [n_layers * (vps[k].shape[3] + (3 + 1) * vhs[k].shape[3]) for k in range(2)]
     sent = sum(sizes) + n_mats * ((TP - 1) * 3 + 1 + 3) * LANES
     wait_bytes(gm_out.at[0, 0, pl.ds(0, sent // LANES)], v_send.at[0])
@@ -546,9 +546,9 @@
             vm((n_m + 2, TP, 1, 2 * LANES), F32), vm((n_m + 2, TP, 1, LANES), F32),
             vm((n_m + 4, 2, 1, LANES), F32), vm((n_m + 2, 4, 1, LANES), F32),
             vm((8, LANES), F32), vm((8, LANES), F32), vm((LANES, LANES), F32),
-            sem((2 + n_m,)), sem((4,)), sem((3,)), sem((PARTS,)), sem((2 + n_m,)),
+            sem((4,)), sem((4,)), sem((3,)), sem((PARTS,)), sem((2 + n_m,)),
             sem((2,)), sem((n_m, 2)), sem((2,)), sem((n_m,)),
-            sem((2,)), sem((PARTS,)), sem((2,)), sem((1,)), sem((3 + 3 * n_m,)),
+            sem((PARTS,)), sem((1,)), sem((3 + 3 * n_m,)),
             pltpu.SemaphoreType.REGULAR((3,)),
         ],
         compiler_params=pltpu.CompilerParams(collective_id=0, has_side_effects=True, vmem_limit_bytes=34 * 2 ** 20),

time: 222 us -> 222 us (level)
  no operation moved by 1% of the time
where the time goes in v5:
time: 222 us
  Pallas kernels  220 us (99%)
  between operations  2.58 us (1%)
    pallas_call x1, Pallas kernels, local_step(): pl.pallas_call(fused_kernel, out_shape=tuple((vm(a.shape, a.dtype) for a...  211 us
    pallas_call x1, Pallas kernels, local_step(): pl.pallas_call(store_kernel, out_shape=tuple((jax.ShapeDtypeStruct(a.shap...  8.89 us

profile of v5, /device:TPU:0, one launch (start us, length us, event | category | flops | bytes accessed | tf_op | source)
XLA Modules:
  0.0 222.2 jit_solution(1613579525593337345)
XLA Ops:
  2.6 210.7 %fused_update.1 = (f32[2,1024,1792]{2,1,0:T(8,128)S(1)}, f32[2,1280,1024]{2,1,0:T(8,128)S(1)}, bf16[2,128,1792]{2,1,0:T(8,128)(2,1)S(1)}, bf16[2,1280,128]{2,1,0...) custom-call(f32[1,2,1024,1792]{3,2,1,0:T(8,128)} %g_in.1, ...), custom_call_target="tpu_custom_call" | custom-call | tf_op jit(solution)/shard_map/fused_update/pallas_call | solution.py:532
  213.3 8.9 %store_out.1 = (f32[2,1024,1792]{2,1,0:T(8,128)}, f32[2,1280,1024]{2,1,0:T(8,128)}, bf16[2,128,1792]{2,1,0:T(8,128)(2,1)}, bf16[2,1280,128]{2,1,0:T(8,128)(2,1)}...) custom-call(f32[2,1024,1792]{2,1,0:T(8,128)S(1)} %get-tuple-element.16.refs_0_, ...), custom_call_target="tpu_custom_call" | custom-call | tf_op jit(solution)/shard_map/store_out/pallas_call | solution.py:557
